TPU v7x, 32 devices: a whole 2x2x4 slice. The times are simulated.
32 devices in a mesh: com: 8 (over y, x, core), arc: 4 (over z).
Axes of the slice: x: 2, y: 2, z: 4, core: 2. Of those that a mesh axis runs over, the one named last changes fastest.
Arguments:
- flow_start: float32 [256, 65536], P('com', 'arc'), may hold values from 0 to 1
- price_start: float32 [256, 16384], P('com'), may hold values from -3 to 3
- cost: float32 [256, 65536], P('com', 'arc'), may hold values from -6 to 6
- demand: float32 [256, 16384], P('com'), may hold values from -6 to 6
- head_block: int32 [512], P('arc'), may hold values from 0 to 127
- tail_block: int32 [512], P('arc'), may hold values from 0 to 127
- head_local: int32 [65536], P('arc'), may hold values from 0 to 127
- tail_local: int32 [65536], P('arc'), may hold values from 0 to 127
- cap_class: int32 [65536], P('arc'), may hold values from 0 to 7
- cap_levels: float32 [8], replicated, may hold values from 25 to 128
Outputs:
- flow: float32 [256, 65536], P('com', 'arc')
- price: float32 [256, 16384], P('com')
Inputs may be any that keep to these rules, and one draw needn't show every extreme that they name: `head_block`: node block indices. `tail_block`: node block indices. `head_local`: positions within a node block. `tail_local`: positions within a node block.
All inputs are finite; a program needn't handle non-finite values.
Results may differ from a plain program's by a relative error of at most 0.00016.
Values sent between devices are 32-bit elements; how exact they have to be, the bound alone decides.
A program may use at most 128 MiB of HBM per device.

v0:
```python
import jax
import jax.numpy as jnp
from jax import lax
from jax.sharding import PartitionSpec as P

NODES = 16384
BLOCK = 128
CLASSES = 8
ITERS = 4
NEWTON = 3
step_primal = 0.25
step_dual = 0.1
soft_width = 0.05
highest = lax.Precision.HIGHEST


def column_sums(values, theta):
    excess = jnp.maximum(values - theta, 0.0)
    return (jnp.sum(excess, axis=0), jnp.sum(jnp.minimum(excess / soft_width, 1.0), axis=0))


def theta_step(theta, total, active, capacity):
    return theta + jnp.maximum(total - capacity, 0.0) / jnp.maximum(active, 1.0)


def on_device(
    flow_start,
    price_start,
    cost,
    demand,
    head_block,
    tail_block,
    head_local,
    tail_local,
    cap_class,
    cap_levels,
):
    com_rows, arc_cols = flow_start.shape
    blocks = arc_cols // BLOCK
    node_blocks = NODES // BLOCK
    lanes = jnp.arange(BLOCK, dtype=jnp.int32)
    head_table = (head_local.reshape(blocks, BLOCK)[:, :, None] == lanes).astype(jnp.float32)
    tail_table = (tail_local.reshape(blocks, BLOCK)[:, :, None] == lanes).astype(jnp.float32)
    block_ids = jnp.arange(node_blocks, dtype=jnp.int32)
    head_owner = (head_block[:, None] == block_ids).astype(jnp.float32)
    tail_owner = (tail_block[:, None] == block_ids).astype(jnp.float32)
    class_ids = jnp.arange(CLASSES, dtype=jnp.int32)
    capacity = jnp.sum(
        jnp.where(cap_class[:, None] == class_ids, cap_levels[None, :], 0.0), axis=1
    ).reshape(blocks, BLOCK)
    flow = flow_start.reshape(com_rows, blocks, BLOCK)
    unit_cost = cost.reshape(com_rows, blocks, BLOCK)
    price = price_start
    for step in range(ITERS):
        grid = price.reshape(com_rows, node_blocks, BLOCK)
        at_head = jnp.einsum("jn,knl->jkl", head_owner, grid, precision=highest)
        at_head = jnp.einsum("jkl,jal->kja", at_head, head_table, precision=highest)
        at_tail = jnp.einsum("jn,knl->jkl", tail_owner, grid, precision=highest)
        at_tail = jnp.einsum("jkl,jal->kja", at_tail, tail_table, precision=highest)
        trial = flow - step_primal * (unit_cost - (at_head - at_tail))
        values = lax.all_to_all(trial, "com", split_axis=1, concat_axis=0, tiled=True)
        limits = lax.all_to_all(capacity[None], "com", split_axis=1, concat_axis=0, tiled=True)
        theta = jnp.zeros(values.shape[1:], jnp.float32)
        for inner in range(NEWTON):
            total, active = column_sums(values, theta)
            theta = theta_step(theta, total, active, limits[0])
        fresh = lax.all_to_all(
            jnp.maximum(values - theta, 0.0), "com", split_axis=0, concat_axis=1, tiled=True
        )
        flows = 2.0 * fresh - flow
        inward = jnp.einsum("kja,jal->jkl", flows, head_table, precision=highest)
        inward = jnp.einsum("jn,jkl->knl", head_owner, inward, precision=highest)
        outward = jnp.einsum("kja,jal->jkl", flows, tail_table, precision=highest)
        outward = jnp.einsum("jn,jkl->knl", tail_owner, outward, precision=highest)
        balance = (inward - outward).reshape(com_rows, NODES)
        summed = lax.psum(balance, "arc")
        price = price + step_dual * (demand - summed)
        flow = fresh
    return (flow.reshape(com_rows, arc_cols), price)


def solution(mesh):
    return jax.shard_map(
        on_device,
        mesh=mesh,
        in_specs=(
            P("com", "arc"),
            P("com", None),
            P("com", "arc"),
            P("com", None),
            P("arc"),
            P("arc"),
            P("arc"),
            P("arc"),
            P("arc"),
            P(),
        ),
        out_specs=(P("com", "arc"), P("com", None)),
        check_vma=False,
    )
```

profile of v0, /device:TPU:0, one launch (start us, length us, event | category | flops | bytes accessed | tf_op | source)
XLA Modules:
  0.0 859.6 jit_solution(16881110937198093419)
XLA Ops:
  11.9 9.8 %fusion.7 = f32[128,128,32]{1,2,0:T(8,128)S(1)} fusion(s32[128,128]{1,0:T(8,128)S(1)} %bitcast.332, f32[128,32,128]{2,0,1:T(8,128)S(1)} %fusion.132), kind=kOutput, calls=%fused_computation.8 | convolution fusion | flops 807403520 | bytes 4259840 | tf_op jit(solution)/shard_map/jkl,jal->kja/dot_general | solution.py:59
  21.8 9.1 %fusion.33 = f32[32,128,128]{2,0,1:T(8,128)} fusion(f32[128,128,32]{1,2,0:T(8,128)S(1)} %fusion.7, f32[128,32,128]{2,0,1:T(8,128)S(1)} %fusion.119, s32[128,128]{1,0:T(8,128)S(1)} %bitcast.323, f32[32,16384]{1,0:T(8,128)S(1)} %copy-done, f32[32,16384]{1,0:T(8,128)S(1)} %copy-done.9), kind=kOutput, calls=%fused_computation.44 | convolution fusion | flops 809500672 | bytes 10551296 | tf_op jit(solution)/shard_map/jkl,jal->kja/dot_general | solution.py:57
  37.1 25.8 %all-to-all-done = f32[32,128,128]{2,0,1:T(8,128)} async-done(((f32[32,128,128]{2,0,1:T(8,128)}), f32[32,128,128]{2,0,1:T(8,128)}, u32[]{:S(2)}, u32[]{:S(2)}) %all-to-all-start) | async-done | bytes 2097184 | tf_op jit(solution)/shard_map/all_to_all | solution.py:61
  80.1 30.6 %all_to_all.168 = f32[256,16,128]{2,1,0:T(8,128)S(1)} all-to-all(f32[256,16,128]{2,1,0:T(8,128)S(1)} %fusion.43), channel_id=1, replica_groups=mesh['com'=8,'arc'=4] {'com'}, dimensions={0} | all-to-all | bytes 4194304 | tf_op jit(solution)/shard_map/all_to_all | solution.py:67
  121.0 7.5 fusion.14
  142.5 86.0 %all-reduce.5.cloned.1.call-done = f32[32,16384]{1,0:T(8,128)} async-done(((f32[32,16384]{1,0:T(8,128)}), f32[32,16384]{1,0:T(8,128)}) %all-reduce.5.cloned.1.call-update) | async-done | bytes 2097168 | tf_op jit(solution)/shard_map/psum | solution.py:76
  234.5 9.8 %fusion.5 = f32[128,128,32]{1,2,0:T(8,128)S(1)} fusion(s32[128,128]{1,0:T(8,128)S(1)} %bitcast.334, f32[128,32,128]{2,0,1:T(8,128)S(1)} %fusion.129), kind=kOutput, calls=%fused_computation.6 | convolution fusion | flops 807403520 | bytes 4259840 | tf_op jit(solution)/shard_map/jkl,jal->kja/dot_general | solution.py:59
  244.3 10.2 %fusion.35 = f32[32,128,128]{2,0,1:T(8,128)S(1)} fusion(f32[32,8,16,128]{3,0,2,1:T(8,128)S(1)} %copy-done.6, f32[128,128,32]{1,2,0:T(8,128)S(1)} %fusion.5, f32[128,32,128]{2,0,1:T(8,128)S(1)} %fusion.116, s32[128,128]{1,0:T(8,128)S(1)} %bitcast.325, f32[32,16384]{1,0:T(8,128)S(1)} %copy-done), kind=kOutput, calls=%fused_computation.46 | convolution fusion | flops 809500672 | bytes 10551296 | tf_op jit(solution)/shard_map/jkl,jal->kja/dot_general | solution.py:57
  254.5 30.0 %all_to_all.169 = f32[32,128,128]{2,0,1:T(8,128)S(1)} all-to-all(f32[32,128,128]{2,0,1:T(8,128)S(1)} %fusion.35), channel_id=1, replica_groups=mesh['com'=8,'arc'=4] {'com'}, dimensions={1} | all-to-all | bytes 4194304 | tf_op jit(solution)/shard_map/all_to_all | solution.py:61
  290.8 29.4 %all_to_all.170 = f32[256,16,128]{2,1,0:T(8,128)S(1)} all-to-all(f32[256,16,128]{2,1,0:T(8,128)S(1)} %fusion.42), channel_id=1, replica_groups=mesh['com'=8,'arc'=4] {'com'}, dimensions={0} | all-to-all | bytes 4194304 | tf_op jit(solution)/shard_map/all_to_all | solution.py:67
  329.6 7.5 fusion.12
  351.0 83.3 %all-reduce.7.cloned.1.call-done = f32[32,16384]{1,0:T(8,128)} async-done(((f32[32,16384]{1,0:T(8,128)}), f32[32,16384]{1,0:T(8,128)}) %all-reduce.7.cloned.1.call-update) | async-done | bytes 2097168 | tf_op jit(solution)/shard_map/psum | solution.py:76
  442.1 9.8 %fusion.3 = f32[128,128,32]{1,2,0:T(8,128)S(1)} fusion(s32[128,128]{1,0:T(8,128)S(1)} %bitcast.336, f32[128,32,128]{2,0,1:T(8,128)S(1)} %fusion.126), kind=kOutput, calls=%fused_computation.4 | convolution fusion | flops 807403520 | bytes 4259840 | tf_op jit(solution)/shard_map/jkl,jal->kja/dot_general | solution.py:59
  451.9 10.2 %fusion.37 = f32[32,128,128]{2,0,1:T(8,128)S(1)} fusion(f32[32,8,16,128]{3,0,2,1:T(8,128)S(1)} %copy-done.4, f32[128,128,32]{1,2,0:T(8,128)S(1)} %fusion.3, f32[128,32,128]{2,0,1:T(8,128)S(1)} %fusion.113, s32[128,128]{1,0:T(8,128)S(1)} %bitcast.327, f32[32,16384]{1,0:T(8,128)S(1)} %copy-done), kind=kOutput, calls=%fused_computation.48 | convolution fusion | flops 809500672 | bytes 10551296 | tf_op jit(solution)/shard_map/jkl,jal->kja/dot_general | solution.py:57
  462.1 30.0 %all_to_all.171 = f32[32,128,128]{2,0,1:T(8,128)S(1)} all-to-all(f32[32,128,128]{2,0,1:T(8,128)S(1)} %fusion.37), channel_id=1, replica_groups=mesh['com'=8,'arc'=4] {'com'}, dimensions={1} | all-to-all | bytes 4194304 | tf_op jit(solution)/shard_map/all_to_all | solution.py:61
  498.4 29.2 %all_to_all.172 = f32[256,16,128]{2,1,0:T(8,128)S(1)} all-to-all(f32[256,16,128]{2,1,0:T(8,128)S(1)} %fusion.41), channel_id=1, replica_groups=mesh['com'=8,'arc'=4] {'com'}, dimensions={0} | all-to-all | bytes 4194304 | tf_op jit(solution)/shard_map/all_to_all | solution.py:67
  537.0 7.5 fusion.10
  558.6 83.1 %all-reduce.9.cloned.1.call-done = f32[32,16384]{1,0:T(8,128)} async-done(((f32[32,16384]{1,0:T(8,128)}), f32[32,16384]{1,0:T(8,128)}) %all-reduce.9.cloned.1.call-update) | async-done | bytes 2097168 | tf_op jit(solution)/shard_map/psum | solution.py:76
  647.7 9.8 %fusion.1 = f32[128,128,32]{1,2,0:T(8,128)S(1)} fusion(s32[128,128]{1,0:T(8,128)S(1)} %bitcast.338, f32[128,32,128]{2,0,1:T(8,128)S(1)} %fusion.123), kind=kOutput, calls=%fused_computation.2 | convolution fusion | flops 807403520 | bytes 4259840 | tf_op jit(solution)/shard_map/jkl,jal->kja/dot_general | solution.py:59
  657.6 10.2 %fusion.39 = f32[32,128,128]{2,0,1:T(8,128)S(1)} fusion(f32[32,8,16,128]{3,0,2,1:T(8,128)S(1)} %copy-done.2, f32[128,128,32]{1,2,0:T(8,128)S(1)} %fusion.1, f32[128,32,128]{2,0,1:T(8,128)S(1)} %fusion.110, s32[128,128]{1,0:T(8,128)S(1)} %bitcast.329, f32[32,16384]{1,0:T(8,128)S(1)} %copy-done), kind=kOutput, calls=%fused_computation.50 | convolution fusion | flops 809500672 | bytes 10551296 | tf_op jit(solution)/shard_map/jkl,jal->kja/dot_general | solution.py:57
  667.8 30.0 %all_to_all.173 = f32[32,128,128]{2,0,1:T(8,128)S(1)} all-to-all(f32[32,128,128]{2,0,1:T(8,128)S(1)} %fusion.39), channel_id=1, replica_groups=mesh['com'=8,'arc'=4] {'com'}, dimensions={1} | all-to-all | bytes 4194304 | tf_op jit(solution)/shard_map/all_to_all | solution.py:61
  704.1 29.2 %all_to_all.174 = f32[256,16,128]{2,1,0:T(8,128)S(1)} all-to-all(f32[256,16,128]{2,1,0:T(8,128)S(1)} %fusion.40), channel_id=1, replica_groups=mesh['com'=8,'arc'=4] {'com'}, dimensions={0} | all-to-all | bytes 4194304 | tf_op jit(solution)/shard_map/all_to_all | solution.py:67
  735.5 7.5 fusion
  768.5 79.2 %all-reduce.11.cloned.1.call-done = f32[32,16384]{1,0:T(8,128)} async-done(((f32[32,16384]{1,0:T(8,128)}), f32[32,16384]{1,0:T(8,128)}) %all-reduce.11.cloned.1.call-update) | async-done | bytes 2097168 | tf_op jit(solution)/shard_map/psum | solution.py:76
  (127 shorter events, 170.3 us)
Async XLA Ops:
  7.2 14.6 %copy-start = (f32[32,16384]{1,0:T(8,128)S(1)}, f32[32,16384]{1,0:T(8,128)}, u32[]{:S(2)}) copy-start(f32[32,16384]{1,0:T(8,128)} %param.12) | copy-start | bytes 6291460
  7.2 2.1 copy-start.15
  9.3 1.3 copy-start.16
  10.6 1.3 copy-start.13
  11.9 9.9 %copy-start.9 = (f32[32,16384]{1,0:T(8,128)S(1)}, f32[32,16384]{1,0:T(8,128)}, u32[]{:S(2)}) copy-start(f32[32,16384]{1,0:T(8,128)} %param.10) | copy-start | bytes 6291460
  11.9 9.9 %copy-start.12 = (s32[16384]{0:T(1024)S(1)}, s32[16384]{0:T(1024)}, u32[]{:S(2)}) copy-start(s32[16384]{0:T(1024)} %param.16) | copy-start | bytes 196612
  30.9 5.3 copy-start.14
  30.9 5.3 copy-start.17
  30.9 32.0 %all-to-all-start = ((f32[32,128,128]{2,0,1:T(8,128)}), f32[32,128,128]{2,0,1:T(8,128)}, u32[]{:S(2)}, u32[]{:S(2)}) async-start(f32[32,128,128]{2,0,1:T(8,128)} %fusion.33), calls=%async_computation | async-start | bytes 4194304 | tf_op jit(solution)/shard_map/all_to_all | solution.py:61
  62.9 10.6 %all-to-all-start.1 = ((f32[1,128,128]{2,0,1:T(1,128)}), f32[1,128,128]{2,0,1:T(1,128)S(1)}, u32[]{:S(2)}, u32[]{:S(2)}) async-start(f32[1,128,128]{2,0,1:T(1,128)} %bitcast.8), calls=%async_computation.1 | async-start | bytes 131072 | tf_op jit(solution)/shard_map/all_to_all | solution.py:62
  66.3 162.1 %all-reduce.5.cloned.1.call-start = ((), (), s32[]{:S(2)}) async-start(), calls=%async_computation.9 | async-start | bytes 4194304 | tf_op jit(solution)/shard_map/psum | solution.py:76
  73.5 6.4 copy-start.11
  110.7 1.6 copy-start.10
  112.3 1.3 copy-start.5
  142.2 292.1 %all-reduce.7.cloned.1.call-start = ((), (), s32[]{:S(2)}) async-start(), calls=%async_computation.10 | async-start | bytes 4194304 | tf_op jit(solution)/shard_map/psum | solution.py:76
  234.5 9.9 %copy-start.6 = (f32[32,8,16,128]{3,0,2,1:T(8,128)S(1)}, f32[32,8,16,128]{3,0,2,1:T(8,128)}, u32[]{:S(2)}) copy-start(f32[32,8,16,128]{3,0,2,1:T(8,128)} %copy-done.5) | copy-start | bytes 6291460
  320.9 1.3 copy-start.3
  350.7 290.9 %all-reduce.9.cloned.1.call-start = ((), (), s32[]{:S(2)}) async-start(), calls=%async_computation.11 | async-start | bytes 4194304 | tf_op jit(solution)/shard_map/psum | solution.py:76
  438.2 1.4 copy-start.7
  442.1 9.9 %copy-start.4 = (f32[32,8,16,128]{3,0,2,1:T(8,128)S(1)}, f32[32,8,16,128]{3,0,2,1:T(8,128)}, u32[]{:S(2)}) copy-start(f32[32,8,16,128]{3,0,2,1:T(8,128)} %copy-done.3) | copy-start | bytes 6291460
  528.3 1.3 copy-start.1
  558.1 289.5 %all-reduce.11.cloned.1.call-start = ((), (), s32[]{:S(2)}) async-start(), calls=%async_computation.12 | async-start | bytes 4194304 | tf_op jit(solution)/shard_map/psum | solution.py:76
  647.7 9.9 %copy-start.2 = (f32[32,8,16,128]{3,0,2,1:T(8,128)S(1)}, f32[32,8,16,128]{3,0,2,1:T(8,128)}, u32[]{:S(2)}) copy-start(f32[32,8,16,128]{3,0,2,1:T(8,128)} %copy-done.1) | copy-start | bytes 6291460
  733.3 1.3 copy-start.8
Sparse Core Ops, SparseCore 0:
  142.3 86.0 all-reduce.4
  350.9 83.3 all-reduce.6
  558.3 83.3 all-reduce.8
  764.3 83.3 all-reduce.10
where the time goes:
time: 868 us; the launch traced here: 860 us
  waiting for transfers between devices  357 us (41%)
  blocking collectives  209 us (24%)
  matrix products  175 us (20%)
  local copies, waits for them, and re-layouts  51.7 us (6%)
  other arithmetic  42.8 us (5%)
  between operations  14.6 us (2%)
  starting transfers between devices  9.63 us (1%)
    psum x4, waiting for transfers between devices, on_device(): summed = lax.psum(balance, 'arc')  332 us
    all_to_all x4, blocking collectives, on_device(): lax.all_to_all(jnp.maximum(values - theta, 0.0), 'com', split_axis=0, con...  118 us
    all_to_all x3, blocking collectives, on_device(): lax.all_to_all(trial, 'com', split_axis=1, concat_axis=0, tiled=True)  90 us
    dot_general x4, matrix products, on_device(): at_head = jnp.einsum('jkl,jal->kja', at_head, head_table, precision=highest)  39.7 us
    dot_general x4, matrix products, on_device(): at_tail = jnp.einsum('jkl,jal->kja', at_tail, tail_table, precision=highest)  39.3 us
    dot_general x4, matrix products, on_device(): inward = jnp.einsum('kja,jal->jkl', flows, head_table, precision=highest)  29.9 us
    dot_general x4, matrix products, on_device(): outward = jnp.einsum('kja,jal->jkl', flows, tail_table, precision=highest)  29.7 us
    unnamed x45, local copies, waits for them, and re-layouts  28 us
  transfers between devices with their start and end apart: 6, of which 5 were waited for; matrix products, arithmetic and copies ran while one was open for 1% of the time, Pallas kernels for 0%

commit v1 on v0

--- a/solution.py
+++ b/solution.py
@@ -2,6 +2,7 @@
 import jax.numpy as jnp
 from jax import lax
 from jax.sharding import PartitionSpec as P
+from jax.lax import all_gather
 
 NODES = 16384
 BLOCK = 128
@@ -73,7 +74,7 @@
         outward = jnp.einsum("kja,jal->jkl", flows, tail_table, precision=highest)
         outward = jnp.einsum("jn,jkl->knl", tail_owner, outward, precision=highest)
         balance = (inward - outward).reshape(com_rows, NODES)
-        summed = lax.psum(balance, "arc")
+        summed = all_gather(balance, axis_name="arc").sum(axis=0)
         price = price + step_dual * (demand - summed)
         flow = fresh
     return (flow.reshape(com_rows, arc_cols), price)

time: 868 us -> 1140 us (1.31)
  waiting for transfers between devices: 357 us -> 609 us
  other arithmetic: 42.8 us -> 64.6 us
    all_gather x0 -> x4, waiting for transfers between devices: none -> 583 us  [on_device(): summed = all_gather(balance, axis_name='arc').sum(axis=0)]
    psum x4 -> x0, waiting for transfers between devices: 332 us -> none  [on_device(): summed = lax.psum(balance, 'arc')]
    reduce_sum x0 -> x4, other arithmetic: none -> 21.8 us  [on_device(): summed = all_gather(balance, axis_name='arc').sum(axis=0)]
    unnamed x45 -> x41, local copies, waits for them, and re-layouts: 28 us -> 11.5 us
where the time goes in v1:
time: 1140 us; the launch traced here: 1130 us
  waiting for transfers between devices  609 us (53%)
  blocking collectives  209 us (18%)
  matrix products  175 us (15%)
  other arithmetic  64.6 us (6%)
  local copies, waits for them, and re-layouts  46.3 us (4%)
  between operations  14.6 us (1%)
    all_gather x4, waiting for transfers between devices, on_device(): summed = all_gather(balance, axis_name='arc').sum(axis=0)  583 us
    all_to_all x4, blocking collectives, on_device(): lax.all_to_all(jnp.maximum(values - theta, 0.0), 'com', split_axis=0, con...  118 us
    all_to_all x3, blocking collectives, on_device(): lax.all_to_all(trial, 'com', split_axis=1, concat_axis=0, tiled=True)  90 us
    dot_general x4, matrix products, on_device(): at_head = jnp.einsum('jkl,jal->kja', at_head, head_table, precision=highest)  39.7 us
    dot_general x4, matrix products, on_device(): at_tail = jnp.einsum('jkl,jal->kja', at_tail, tail_table, precision=highest)  39.3 us
    dot_general x4, matrix products, on_device(): inward = jnp.einsum('kja,jal->jkl', flows, head_table, precision=highest)  29.9 us
    dot_general x4, matrix products, on_device(): outward = jnp.einsum('kja,jal->jkl', flows, tail_table, precision=highest)  29.7 us
    all_to_all x1, waiting for transfers between devices, on_device(): lax.all_to_all(trial, 'com', split_axis=1, concat_axis=0, tiled=True)  25.8 us
  transfers between devices with their start and end apart: 6, of which 5 were waited for; matrix products, arithmetic and copies ran while one was open for 1% of the time, Pallas kernels for 0%

profile of v1, /device:TPU:0, one launch (start us, length us, event | category | flops | bytes accessed | tf_op | source)
XLA Modules:
  0.0 1127.4 jit_solution(321184487123679391)
XLA Ops:
  11.9 9.8 fusion.7
  21.8 9.1 fusion.33
  37.1 25.8 %all-to-all-done = f32[32,128,128]{2,0,1:T(8,128)} async-done(((f32[32,128,128]{2,0,1:T(8,128)}), f32[32,128,128]{2,0,1:T(8,128)}, u32[]{:S(2)}, u32[]{:S(2)}) %all-to-all-start) | async-done | bytes 2097184 | tf_op jit(solution)/shard_map/all_to_all | solution.py:62
  80.1 30.6 %all_to_all.168 = f32[256,16,128]{2,1,0:T(8,128)S(1)} all-to-all(f32[256,16,128]{2,1,0:T(8,128)S(1)} %fusion.43), channel_id=1, replica_groups=mesh['com'=8,'arc'=4] {'com'}, dimensions={0} | all-to-all | bytes 4194304 | tf_op jit(solution)/shard_map/all_to_all | solution.py:68
  121.0 7.5 fusion.14
  141.1 149.4 %all-gather.5.cloned.1.call-done = f32[4,32,16384]{2,1,0:T(8,128)} async-done(((f32[1,32,16384]{2,1,0:T(8,128)}), f32[4,32,16384]{2,1,0:T(8,128)}) %all-gather.5.cloned.1.call-update) | async-done | bytes 8388624 | tf_op jit(solution)/shard_map/all_gather | solution.py:77
  302.0 9.8 fusion.5
  311.8 10.2 fusion.35
  322.0 30.0 %all_to_all.169 = f32[32,128,128]{2,0,1:T(8,128)S(1)} all-to-all(f32[32,128,128]{2,0,1:T(8,128)S(1)} %fusion.35), channel_id=1, replica_groups=mesh['com'=8,'arc'=4] {'com'}, dimensions={1} | all-to-all | bytes 4194304 | tf_op jit(solution)/shard_map/all_to_all | solution.py:62
  358.3 29.4 %all_to_all.170 = f32[256,16,128]{2,1,0:T(8,128)S(1)} all-to-all(f32[256,16,128]{2,1,0:T(8,128)S(1)} %fusion.42), channel_id=1, replica_groups=mesh['com'=8,'arc'=4] {'com'}, dimensions={0} | all-to-all | bytes 4194304 | tf_op jit(solution)/shard_map/all_to_all | solution.py:68
  397.1 7.5 fusion.12
  417.2 145.9 %all-gather.7.cloned.1.call-done = f32[4,32,16384]{2,1,0:T(8,128)} async-done(((f32[1,32,16384]{2,1,0:T(8,128)}), f32[4,32,16384]{2,1,0:T(8,128)}) %all-gather.7.cloned.1.call-update) | async-done | bytes 8388624 | tf_op jit(solution)/shard_map/all_gather | solution.py:77
  576.5 9.8 fusion.3
  586.3 10.2 fusion.37
  596.5 30.0 %all_to_all.171 = f32[32,128,128]{2,0,1:T(8,128)S(1)} all-to-all(f32[32,128,128]{2,0,1:T(8,128)S(1)} %fusion.37), channel_id=1, replica_groups=mesh['com'=8,'arc'=4] {'com'}, dimensions={1} | all-to-all | bytes 4194304 | tf_op jit(solution)/shard_map/all_to_all | solution.py:62
  632.8 29.2 %all_to_all.172 = f32[256,16,128]{2,1,0:T(8,128)S(1)} all-to-all(f32[256,16,128]{2,1,0:T(8,128)S(1)} %fusion.41), channel_id=1, replica_groups=mesh['com'=8,'arc'=4] {'com'}, dimensions={0} | all-to-all | bytes 4194304 | tf_op jit(solution)/shard_map/all_to_all | solution.py:68
  671.4 7.5 fusion.10
  691.7 145.7 %all-gather.9.cloned.1.call-done = f32[4,32,16384]{2,1,0:T(8,128)} async-done(((f32[1,32,16384]{2,1,0:T(8,128)}), f32[4,32,16384]{2,1,0:T(8,128)}) %all-gather.9.cloned.1.call-update) | async-done | bytes 8388624 | tf_op jit(solution)/shard_map/all_gather | solution.py:77
  848.8 9.8 fusion.1
  858.7 10.2 fusion.39
  868.9 30.0 %all_to_all.173 = f32[32,128,128]{2,0,1:T(8,128)S(1)} all-to-all(f32[32,128,128]{2,0,1:T(8,128)S(1)} %fusion.39), channel_id=1, replica_groups=mesh['com'=8,'arc'=4] {'com'}, dimensions={1} | all-to-all | bytes 4194304 | tf_op jit(solution)/shard_map/all_to_all | solution.py:62
  905.2 29.2 %all_to_all.174 = f32[256,16,128]{2,1,0:T(8,128)S(1)} all-to-all(f32[256,16,128]{2,1,0:T(8,128)S(1)} %fusion.40), channel_id=1, replica_groups=mesh['com'=8,'arc'=4] {'com'}, dimensions={0} | all-to-all | bytes 4194304 | tf_op jit(solution)/shard_map/all_to_all | solution.py:68
  936.6 7.5 fusion
  968.2 141.8 %all-gather.11.cloned.1.call-done = f32[4,32,16384]{2,1,0:T(8,128)} async-done(((f32[1,32,16384]{2,1,0:T(8,128)}), f32[4,32,16384]{2,1,0:T(8,128)}) %all-gather.11.cloned.1.call-update) | async-done | bytes 8388624 | tf_op jit(solution)/shard_map/all_gather | solution.py:77
  (131 shorter events, 186.8 us)
Async XLA Ops:
  7.2 14.6 %copy-start = (f32[32,16384]{1,0:T(8,128)S(1)}, f32[32,16384]{1,0:T(8,128)}, u32[]{:S(2)}) copy-start(f32[32,16384]{1,0:T(8,128)} %param.12) | copy-start | bytes 6291460
  7.2 2.1 copy-start.15
  9.3 1.3 copy-start.16
  10.6 1.3 copy-start.13
  11.9 9.9 copy-start.9
  11.9 9.9 copy-start.12
  30.9 5.3 copy-start.14
  30.9 5.3 copy-start.17
  30.9 32.0 %all-to-all-start = ((f32[32,128,128]{2,0,1:T(8,128)}), f32[32,128,128]{2,0,1:T(8,128)}, u32[]{:S(2)}, u32[]{:S(2)}) async-start(f32[32,128,128]{2,0,1:T(8,128)} %fusion.33), calls=%async_computation | async-start | bytes 4194304 | tf_op jit(solution)/shard_map/all_to_all | solution.py:62
  62.9 10.6 all-to-all-start.1
  66.3 224.2 %all-gather.5.cloned.1.call-start = ((), (), s32[]{:S(2)}) async-start(), calls=%async_computation.9 | async-start | bytes 10485760 | tf_op jit(solution)/shard_map/all_gather | solution.py:77
  73.5 6.4 copy-start.11
  110.7 1.6 copy-start.10
  112.3 1.3 copy-start.5
  140.8 422.3 %all-gather.7.cloned.1.call-start = ((), (), s32[]{:S(2)}) async-start(), calls=%async_computation.10 | async-start | bytes 10485760 | tf_op jit(solution)/shard_map/all_gather | solution.py:77
  302.0 9.9 copy-start.6
  388.4 1.3 copy-start.3
  417.0 420.4 %all-gather.9.cloned.1.call-start = ((), (), s32[]{:S(2)}) async-start(), calls=%async_computation.11 | async-start | bytes 10485760 | tf_op jit(solution)/shard_map/all_gather | solution.py:77
  572.5 1.4 copy-start.7
  576.4 9.9 copy-start.4
  662.7 1.3 copy-start.1
  691.2 418.8 %all-gather.11.cloned.1.call-start = ((), (), s32[]{:S(2)}) async-start(), calls=%async_computation.12 | async-start | bytes 10485760 | tf_op jit(solution)/shard_map/all_gather | solution.py:77
  848.8 9.9 copy-start.2
  934.4 1.3 copy-start.8
Sparse Core Ops, SparseCore 0:
  140.9 149.5 all-gather.4
  417.1 145.9 all-gather.6
  691.3 145.9 all-gather.8
  964.0 145.9 all-gather.10
